TPU v7x, 32 devices: a whole 2x2x4 slice. The times are simulated.
32 devices in a mesh: row: 4 (over y, x), col: 8 (over z, core).
Axes of the slice: x: 2, y: 2, z: 4, core: 2. Of those that a mesh axis runs over, the one named last changes fastest.
Arguments:
- fire_state: float32 [64, 192, 1024], P(None, 'row', 'col'), may hold values from -6 to 6
- fuel_class: int32 [192, 1024], P('row', 'col'), may hold values from 0 to 12
- firebreak: int32 [192, 1024], P('row', 'col'), may hold values 0 or 1
- ignition: int32 [192, 1024], P('row', 'col'), may hold values 0 or 1
- spread_rate: float32 [13, 64], replicated, may hold values from 0.03 to 0.12
- spread_rows: float32 [64, 64], replicated, may hold values from -0.375 to 0.375
- spread_cols: float32 [64, 64], replicated, may hold values from -0.375 to 0.375
- reaction: float32 [64, 64], replicated, may hold values from -0.75 to 0.75
- ignition_heat: float32 [64], replicated, may hold values from -4 to 4
Outputs:
- final_state: float32 [64, 192, 1024], P(None, 'row', 'col')
All inputs are finite; a program needn't handle non-finite values. No bound on the sum of `firebreak` or of `ignition` on one device may be relied on, other than what follows from the above.
Results may differ from a plain program's by a relative error of at most 0.0003.
Values sent between devices are 32-bit elements; how exact they have to be, the bound alone decides.
A program may use at most 64 MiB of HBM per device.

v0:
```python
import functools

import jax
import jax.numpy as jnp
from jax import lax
from jax.experimental import pallas as pl
from jax.experimental.pallas import tpu as pltpu
from jax.sharding import PartitionSpec as P

ITERS = 4
PAD = 8
BLOCK = 4
BF16, F32 = jnp.bfloat16, jnp.float32
MESH = pl.DeviceIdType.MESH


def split(x):
    high = x.astype(BF16)
    return high, (x - high.astype(F32)).astype(BF16)


def dot(a, b):
    return jnp.dot(a, b, preferred_element_type=F32)


def lanes(shape):
    return lax.broadcasted_iota(jnp.int32, shape, 1)


def rows_of(shape):
    return lax.broadcasted_iota(jnp.int32, shape, 0)


def on_diagonal(matrix):
    c = matrix.shape[0]
    turned = matrix.T
    wide = jnp.concatenate([turned, turned], axis=1)
    first = lanes(wide.shape) < c
    return jnp.concatenate([jnp.where(first, wide, 0.0), jnp.where(first, 0.0, wide)], axis=0)


def kernel(
    dims,
    x_ref, fuel_ref, break_ref, lit_ref, rate_ref, srow_ref, scol_ref, react_ref, heat_ref,
    out_ref,
    v, mid, local, coef, burn, heat, gr, gc, w1, w2, w3, wc, send_row, send_col, recv_row, recv_col, send_sem, recv_sem,
):
    n_row, n_col, c, h, w, k8 = dims
    p_all, half = h // 2, w // 2
    two = 2 * c
    r, q = lax.axis_index("row"), lax.axis_index("col")
    has_up, has_down = r > 0, r < n_row - 1
    has_left, has_right = q > 0, q < n_col - 1
    partner = ({"row": r - 1}, {"row": r + 1}, {"col": q - 1}, {"col": q + 1})
    sends = (has_up, has_down, has_left, has_right)
    takes = (has_down, has_up, has_right, has_left)

    recv_row[...] = jnp.zeros_like(recv_row)
    recv_col[...] = jnp.zeros_like(recv_col)
    barrier = pltpu.get_barrier_semaphore()
    for d in range(4):
        @pl.when(sends[d])
        def _(d=d):
            pl.semaphore_signal(barrier, inc=1, device_id=partner[d], device_id_type=MESH)

    def copy(slot, d):
        src, dst = (send_row, recv_row) if d < 2 else (send_col, recv_col)
        return pltpu.make_async_remote_copy(
            src_ref=src.at[slot, d % 2],
            dst_ref=dst.at[slot, d % 2],
            send_sem=send_sem.at[slot, d],
            recv_sem=recv_sem.at[slot, d],
            device_id=partner[d],
            device_id_type=MESH,
        )

    def start(slot, d):
        @pl.when(sends[d])
        def _():
            copy(slot, d).start()

    def finish(slot):
        for d in range(4):
            @pl.when(sends[d])
            def _(d=d):
                copy(slot, d).wait_send()
        for d in range(4):
            @pl.when(takes[d])
            def _(d=d):
                copy(slot, d).wait_recv()

    first_half = lanes((half, two)) < c

    def send_rows(slot, top, bottom):
        send_row[slot, 0] = jnp.where(first_half, top[:half], pltpu.roll(top[half:], c, axis=1))
        send_row[slot, 1] = jnp.where(first_half, pltpu.roll(bottom[:half], c, axis=1), bottom[half:])
        start(slot, 0)
        start(slot, 1)

    def turn_in(p):
        tall = jnp.concatenate([x_ref[pl.ds(p, c, stride=h), :], x_ref[pl.ds(p + p_all, c, stride=h), :]], axis=0)
        v[p] = tall.T

    def turn_in_loop(p, carry):
        turn_in(p)
        return carry

    lax.fori_loop(0, p_all, turn_in_loop, 0, unroll=4)

    def column(ref, at):
        size = ref.shape[1]
        flat = ref.reshape(ref.shape[0] * size, two)
        return lambda p: flat[pl.ds(p * size + at, p_all, stride=size), :]

    def send_cols(slot, left, right):
        send_col[slot, 0] = left
        send_col[slot, 1] = right
        start(slot, 2)
        start(slot, 3)

    n_near = sum(s.astype(jnp.int32) for s in sends)
    pl.semaphore_wait(barrier, n_near)
    send_rows(0, v[0], v[p_all - 1])
    send_cols(0, column(v, 0)(0), column(v, w - 1)(0))

    eye = (rows_of((two, two)) == lanes((two, two))).astype(F32)
    row_hi, row_lo = split(eye + on_diagonal(srow_ref[...]))
    col_hi, col_lo = split(eye + on_diagonal(scol_ref[...]))
    rea_hi, rea_lo = split(on_diagonal(react_ref[...]))
    both_hi = jnp.concatenate([row_hi, col_hi], axis=1)
    w1[0:two] = both_hi
    w1[two:2 * two] = both_hi
    w2[...] = jnp.concatenate([row_lo, col_lo], axis=1)
    w3[0:two] = jnp.concatenate([rea_hi, rea_lo], axis=1)
    w3[two:2 * two] = jnp.concatenate([rea_hi, jnp.zeros_like(rea_lo)], axis=1)

    k = rate_ref.shape[0]
    part = k8 + 8
    rates = jnp.concatenate([rate_ref[...], rate_ref[...]], axis=1)
    heats = jnp.concatenate([heat_ref[...], heat_ref[...]], axis=1)
    wc[...] = jnp.zeros_like(wc)
    for s in range(2):
        mine = (lanes((1, two)) < c) if s == 0 else (lanes((1, two)) >= c)
        wc[s * part:s * part + k, 0:two] = jnp.where(mine, rates, 0.0)
        wc[s * part + k8:s * part + k8 + 1, two:2 * two] = jnp.where(mine, 1.0, 0.0)
        wc[s * part + k8 + 1:s * part + k8 + 2, 2 * two:3 * two] = jnp.where(mine, heats, 0.0)
    tables = jnp.concatenate(split(wc[...]), axis=0)
    classes, slots = rows_of((k8, w)), rows_of((8, w))

    def cells(p, carry):
        parts = []
        for s in range(2):
            at = pl.ds(p + s * p_all, 1)
            alive = 1.0 - break_ref[at, :].astype(F32)
            lit = alive * lit_ref[at, :].astype(F32)
            parts.append(jnp.where(fuel_ref[at, :] == classes, alive, 0.0))
            parts.append(jnp.where(slots == 0, alive, jnp.where(slots == 1, lit, 0.0)))
        tall = jnp.concatenate(parts + parts, axis=0)
        terms = dot(tall.T.astype(BF16), tables)
        coef[p] = terms[:, 0:two]
        burn[p] = terms[:, two:2 * two]
        heat[p] = terms[:, 2 * two:3 * two]
        return carry

    lax.fori_loop(0, p_all, cells, 0, unroll=4)

    def spreads(x):
        hi, lo = split(x)
        return dot(jnp.concatenate([hi, lo], axis=1), w1[...]) + dot(hi, w2[...])

    def pointwise(cur, second):
        def body(b, carry):
            at = pl.ds(b * BLOCK, BLOCK)
            x = cur[at].reshape(BLOCK * w, two)
            g = spreads(x)
            g_row, g_col = g[:, :two], g[:, two:]
            hi, lo = split(jnp.tanh(x))
            both = dot(jnp.concatenate([hi, lo], axis=1), w3[...])
            burning = both[:, :two] + both[:, two:]
            flat = lambda ref: ref[at].reshape(BLOCK * w, two)
            fire = flat(burn) * burning + flat(heat) - 2.0 * (flat(coef) * (g_row + g_col)) + 0.5 * x
            if second:
                fire = 0.5 * (fire + flat(v))
            gr[pl.ds(b * BLOCK + 1, BLOCK)] = g_row.reshape(BLOCK, w, two)
            gc[at, PAD:PAD + w] = g_col.reshape(BLOCK, w, two)
            local[at] = fire.reshape(BLOCK, w, two)
            return carry

        lax.fori_loop(0, p_all // BLOCK, body, 0)

    def halo(slot):
        stacked = jnp.concatenate([recv_row[slot, 0], recv_row[slot, 1], recv_col[slot, 0], recv_col[slot, 1]], axis=0)
        g = spreads(stacked)
        below, above = g[0:half, :two], g[half:w, :two]
        last, top = gr[p_all], gr[1]
        wide_first = lanes((w, two)) < c
        over = jnp.concatenate([above, pltpu.roll(above, c, axis=1)], axis=0)
        under = jnp.concatenate([pltpu.roll(below, c, axis=1), below], axis=0)
        gr[0] = jnp.where(wide_first, over, pltpu.roll(last, c, axis=1))
        gr[p_all + 1] = jnp.where(wide_first, pltpu.roll(top, c, axis=1), under)
        flat = gc.reshape(p_all * (w + 2 * PAD), two)
        flat[pl.ds(PAD + w, p_all, stride=w + 2 * PAD), :] = g[w:w + p_all, two:]
        flat[pl.ds(PAD - 1, p_all, stride=w + 2 * PAD), :] = g[w + p_all:w + 2 * p_all, two:]

    def combine(slot, target, second, last):
        def value(p):
            near = (gr[p] + gr[p + 2]) + (gc[p, PAD - 1:PAD - 1 + w] + gc[p, PAD + 1:PAD + 1 + w])
            if second:
                near = 0.5 * near
            return local[p] + coef[p] * near

        def edge(at):
            near = (column(gr, at)(0) + column(gr, at)(2)) + (column(gc, PAD - 1 + at)(0) + column(gc, PAD + 1 + at)(0))
            if second:
                near = 0.5 * near
            return column(local, at)(0) + column(coef, at)(0) * near

        top, bottom = value(0), value(p_all - 1)
        target[0] = top
        target[p_all - 1] = bottom

        def edges():
            send_rows(slot, top, bottom)
            send_cols(slot, edge(0), edge(w - 1))

        if last is None:
            edges()
        else:
            pl.when(jnp.logical_not(last))(edges)

        def body(p, carry):
            target[p] = value(p)
            return carry

        lax.fori_loop(1, p_all - 1, body, 0, unroll=2)

    def step(i, carry):
        pointwise(v, False)
        finish(0)
        halo(0)
        combine(1, mid, False, None)
        pointwise(mid, True)
        finish(1)
        halo(1)
        combine(0, v, True, i == ITERS - 1)
        return carry

    lax.fori_loop(0, ITERS, step, 0)

    def turn_out(p, carry):
        tall = v[p].T
        out_ref[pl.ds(p, c, stride=h), :] = tall[:c]
        out_ref[pl.ds(p + p_all, c, stride=h), :] = tall[c:]
        return carry

    lax.fori_loop(0, p_all, turn_out, 0, unroll=4)


def per_device(n_row, n_col, fire_state, fuel_class, firebreak, ignition, spread_rate, spread_rows, spread_cols, reaction, ignition_heat):
    c, h, w = fire_state.shape
    k = spread_rate.shape[0]
    k8 = -(-k // 8) * 8
    p_all, two = h // 2, 2 * c
    vmem = pl.BlockSpec(memory_space=pltpu.VMEM)
    field = pltpu.VMEM((p_all, w, two), F32)
    out = pl.pallas_call(
        functools.partial(kernel, (n_row, n_col, c, h, w, k8)),
        out_shape=jax.ShapeDtypeStruct((c * h, w), F32),
        in_specs=[vmem] * 9,
        out_specs=vmem,
        scratch_shapes=[
            field, field, field, field, field, field,
            pltpu.VMEM((p_all + 2, w, two), F32),
            pltpu.VMEM((p_all, w + 2 * PAD, two), F32),
            pltpu.VMEM((2 * two, 2 * two), BF16),
            pltpu.VMEM((two, 2 * two), BF16),
            pltpu.VMEM((2 * two, 2 * two), BF16),
            pltpu.VMEM((2 * (k8 + 8), 3 * two), F32),
            pltpu.VMEM((2, 2, w // 2, two), F32),
            pltpu.VMEM((2, 2, p_all, two), F32),
            pltpu.VMEM((2, 2, w // 2, two), F32),
            pltpu.VMEM((2, 2, p_all, two), F32),
            pltpu.SemaphoreType.DMA((2, 4)),
            pltpu.SemaphoreType.DMA((2, 4)),
        ],
        compiler_params=pltpu.CompilerParams(collective_id=0, has_side_effects=True, vmem_limit_bytes=48 * 1024 * 1024),
    )(
        fire_state.reshape(c * h, w), fuel_class, firebreak, ignition,
        spread_rate, spread_rows, spread_cols, reaction, ignition_heat.reshape(1, c),
    )
    return out.reshape(c, h, w)


def solution(mesh):
    grid = P("row", "col")
    field = P(None, "row", "col")
    return jax.shard_map(
        functools.partial(per_device, mesh.shape["row"], mesh.shape["col"]),
        mesh=mesh,
        in_specs=(field, grid, grid, grid, P(), P(), P(), P(), P()),
        out_specs=field,
        check_vma=False,
    )
```

profile of v0, /device:TPU:0, one launch (start us, length us, event | category | flops | bytes accessed | tf_op | source)
XLA Modules:
  0.0 45.0 jit_solution(5831837657845361411)
XLA Ops:
  0.0 0.0 copy-start
  0.0 1.4 %copy-done = f32[64,48,128]{2,1,0:T(8,128)S(1)} copy-done((f32[64,48,128]{2,1,0:T(8,128)S(1)}, f32[64,48,128]{2,1,0:T(8,128)}, u32[]{:S(2)}) %copy-start) | copy-done | bytes 1572888
  1.4 0.0 copy-start.1
  1.4 0.8 %copy-done.1 = f32[64,64]{1,0:T(8,128)S(1)} copy-done((f32[64,64]{1,0:T(8,128)S(1)}, f32[64,64]{1,0:T(8,128)}, u32[]{:S(2)}) %copy-start.1) | copy-done | bytes 16408
  2.2 0.0 copy-start.2
  2.2 0.8 %copy-done.2 = f32[64,64]{1,0:T(8,128)S(1)} copy-done((f32[64,64]{1,0:T(8,128)S(1)}, f32[64,64]{1,0:T(8,128)}, u32[]{:S(2)}) %copy-start.2) | copy-done | bytes 16408
  2.9 0.0 copy-start.3
  2.9 0.8 %copy-done.3 = f32[64,64]{1,0:T(8,128)S(1)} copy-done((f32[64,64]{1,0:T(8,128)S(1)}, f32[64,64]{1,0:T(8,128)}, u32[]{:S(2)}) %copy-start.3) | copy-done | bytes 16408
  3.7 0.0 copy-start.4
  3.7 0.7 %copy-done.4 = s32[48,128]{1,0:T(8,128)S(1)} copy-done((s32[48,128]{1,0:T(8,128)S(1)}, s32[48,128]{1,0:T(8,128)}, u32[]{:S(2)}) %copy-start.4) | copy-done | bytes 24600
  4.4 0.0 copy-start.5
  4.4 0.7 %copy-done.5 = s32[48,128]{1,0:T(8,128)S(1)} copy-done((s32[48,128]{1,0:T(8,128)S(1)}, s32[48,128]{1,0:T(8,128)}, u32[]{:S(2)}) %copy-start.5) | copy-done | bytes 24600
  5.2 0.0 copy-start.6
  5.2 0.7 %copy-done.6 = s32[48,128]{1,0:T(8,128)S(1)} copy-done((s32[48,128]{1,0:T(8,128)S(1)}, s32[48,128]{1,0:T(8,128)}, u32[]{:S(2)}) %copy-start.6) | copy-done | bytes 24600
  5.9 0.0 copy-start.7
  5.9 0.7 %copy-done.7 = f32[13,64]{1,0:T(8,128)S(1)} copy-done((f32[13,64]{1,0:T(8,128)S(1)}, f32[13,64]{1,0:T(8,128)}, u32[]{:S(2)}) %copy-start.7) | copy-done | bytes 3352
  6.6 0.0 copy-start.8
  6.6 0.7 %copy-done.8 = f32[64]{0:T(128)S(1)} copy-done((f32[64]{0:T(128)S(1)}, f32[64]{0:T(128)}, u32[]{:S(2)}) %copy-start.8) | copy-done | bytes 280
  7.3 36.6 %shard_map.91 = f32[3072,128]{1,0:T(8,128)S(1)} custom-call(f32[3072,128]{1,0:T(8,128)S(1)} %bitcast.4, s32[48,128]{1,0:T(8,128)S(1)} %copy-done.4, s32[48,128]{1,0:T(8,128)S(1)} %copy-done.5, s32[48,128]{1,0:T(8,128)S(1)} %copy-done.6, f32[13,64]{1,0:T(8,128)S(1)} %copy-done.7, f32[64,64]{1,0:T(8,128)S(1)} %copy-done.1, f32[64,64]{1,0:T(8,128)S(1)} %copy-done.2, ...), custom_call_target="tpu_custom_call" | custom-call | tf_op jit(solution)/shard_map/pallas_call | solution.py:266
  43.9 1.1 %copy.11 = f32[64,48,128]{2,1,0:T(8,128)} copy(f32[64,48,128]{2,1,0:T(8,128)S(1)} %bitcast.3) | data formatting | bytes 3145728
Async XLA Ops:
  0.0 1.4 %copy-start = (f32[64,48,128]{2,1,0:T(8,128)S(1)}, f32[64,48,128]{2,1,0:T(8,128)}, u32[]{:S(2)}) copy-start(f32[64,48,128]{2,1,0:T(8,128)} %param.9) | copy-start | bytes 4718596
  1.4 0.8 %copy-start.1 = (f32[64,64]{1,0:T(8,128)S(1)}, f32[64,64]{1,0:T(8,128)}, u32[]{:S(2)}) copy-start(f32[64,64]{1,0:T(8,128)} %srow_ref.1) | copy-start | bytes 49156
  2.2 0.8 %copy-start.2 = (f32[64,64]{1,0:T(8,128)S(1)}, f32[64,64]{1,0:T(8,128)}, u32[]{:S(2)}) copy-start(f32[64,64]{1,0:T(8,128)} %scol_ref.1) | copy-start | bytes 49156
  2.9 0.8 %copy-start.3 = (f32[64,64]{1,0:T(8,128)S(1)}, f32[64,64]{1,0:T(8,128)}, u32[]{:S(2)}) copy-start(f32[64,64]{1,0:T(8,128)} %react_ref.1) | copy-start | bytes 49156
  3.7 0.7 %copy-start.4 = (s32[48,128]{1,0:T(8,128)S(1)}, s32[48,128]{1,0:T(8,128)}, u32[]{:S(2)}) copy-start(s32[48,128]{1,0:T(8,128)} %fuel_ref.1) | copy-start | bytes 73732
  4.4 0.7 %copy-start.5 = (s32[48,128]{1,0:T(8,128)S(1)}, s32[48,128]{1,0:T(8,128)}, u32[]{:S(2)}) copy-start(s32[48,128]{1,0:T(8,128)} %break_ref.1) | copy-start | bytes 73732
  5.2 0.7 %copy-start.6 = (s32[48,128]{1,0:T(8,128)S(1)}, s32[48,128]{1,0:T(8,128)}, u32[]{:S(2)}) copy-start(s32[48,128]{1,0:T(8,128)} %lit_ref.1) | copy-start | bytes 73732
  5.9 0.7 %copy-start.7 = (f32[13,64]{1,0:T(8,128)S(1)}, f32[13,64]{1,0:T(8,128)}, u32[]{:S(2)}) copy-start(f32[13,64]{1,0:T(8,128)} %rate_ref.1) | copy-start | bytes 9988
  6.6 0.7 %copy-start.8 = (f32[64]{0:T(128)S(1)}, f32[64]{0:T(128)}, u32[]{:S(2)}) copy-start(f32[64]{0:T(128)} %param.17) | copy-start | bytes 772
where the time goes:
time: 45.6 us; the launch traced here: 45 us
  Pallas kernels  36.6 us (80%)
  local copies, waits for them, and re-layouts  8.39 us (18%)
    pallas_call x1, Pallas kernels, per_device(): pl.pallas_call(functools.partial(kernel, (n_row, n_col, c, h, w, k8)), ou...  36.6 us
    unnamed x19, local copies, waits for them, and re-layouts  8.39 us

commit v1 on v0

--- a/solution.py
+++ b/solution.py
@@ -41,8 +41,9 @@
 
 def kernel(
     dims,
-    x_ref, fuel_ref, break_ref, lit_ref, rate_ref, srow_ref, scol_ref, react_ref, heat_ref,
+    x_hbm, fuel_hbm, break_hbm, lit_hbm, rate_hbm, srow_hbm, scol_hbm, react_hbm, heat_hbm,
     out_ref,
+    x_ref, fuel_ref, break_ref, lit_ref, rate_ref, srow_ref, scol_ref, react_ref, heat_ref, ends_ref, load_sem,
     v, mid, local, coef, burn, heat, gr, gc, w1, w2, w3, wc, send_row, send_col, recv_row, recv_col, send_sem, recv_sem,
 ):
     n_row, n_col, c, h, w, k8 = dims
@@ -55,6 +56,19 @@
     sends = (has_up, has_down, has_left, has_right)
     takes = (has_down, has_up, has_right, has_left)
 
+    def load(n, src, dst):
+        return pltpu.make_async_copy(src, dst, load_sem.at[n])
+
+    end_loads = [load(0, x_hbm.at[:, 0, :], ends_ref.at[0]), load(1, x_hbm.at[:, h - 1, :], ends_ref.at[1])]
+    weight_loads = [load(2, srow_hbm, srow_ref), load(3, scol_hbm, scol_ref), load(4, react_hbm, react_ref)]
+    field_load = load(5, x_hbm, x_ref.reshape(c, h, w))
+    cell_loads = [
+        load(6, fuel_hbm, fuel_ref), load(7, break_hbm, break_ref), load(8, lit_hbm, lit_ref),
+        load(9, rate_hbm, rate_ref), load(10, heat_hbm, heat_ref),
+    ]
+    for one in end_loads + weight_loads + [field_load] + cell_loads:
+        one.start()
+
     recv_row[...] = jnp.zeros_like(recv_row)
     recv_col[...] = jnp.zeros_like(recv_col)
     barrier = pltpu.get_barrier_semaphore()
@@ -94,8 +108,17 @@
     def send_rows(slot, top, bottom):
         send_row[slot, 0] = jnp.where(first_half, top[:half], pltpu.roll(top[half:], c, axis=1))
         send_row[slot, 1] = jnp.where(first_half, pltpu.roll(bottom[:half], c, axis=1), bottom[half:])
-        start(slot, 0)
-        start(slot, 1)
+        odd = lax.rem(r, 2) == 1
+
+        @pl.when(odd)
+        def _():
+            start(slot, 1)
+            start(slot, 0)
+
+        @pl.when(jnp.logical_not(odd))
+        def _():
+            start(slot, 0)
+            start(slot, 1)
 
     def turn_in(p):
         tall = jnp.concatenate([x_ref[pl.ds(p, c, stride=h), :], x_ref[pl.ds(p + p_all, c, stride=h), :]], axis=0)
@@ -104,8 +127,6 @@
     def turn_in_loop(p, carry):
         turn_in(p)
         return carry
-
-    lax.fori_loop(0, p_all, turn_in_loop, 0, unroll=4)
 
     def column(ref, at):
         size = ref.shape[1]
@@ -119,10 +140,14 @@
         start(slot, 3)
 
     n_near = sum(s.astype(jnp.int32) for s in sends)
+    for one in end_loads:
+        one.wait()
+    ends = jnp.concatenate([ends_ref[0], ends_ref[1]], axis=0).T
     pl.semaphore_wait(barrier, n_near)
-    send_rows(0, v[0], v[p_all - 1])
-    send_cols(0, column(v, 0)(0), column(v, w - 1)(0))
-
+    send_rows(0, ends, ends)
+
+    for one in weight_loads:
+        one.wait()
     eye = (rows_of((two, two)) == lanes((two, two))).astype(F32)
     row_hi, row_lo = split(eye + on_diagonal(srow_ref[...]))
     col_hi, col_lo = split(eye + on_diagonal(scol_ref[...]))
@@ -133,6 +158,12 @@
     w2[...] = jnp.concatenate([row_lo, col_lo], axis=1)
     w3[0:two] = jnp.concatenate([rea_hi, rea_lo], axis=1)
     w3[two:2 * two] = jnp.concatenate([rea_hi, jnp.zeros_like(rea_lo)], axis=1)
+
+    field_load.wait()
+    lax.fori_loop(0, p_all, turn_in_loop, 0, unroll=4)
+    send_cols(0, column(v, 0)(0), column(v, w - 1)(0))
+    for one in cell_loads:
+        one.wait()
 
     k = rate_ref.shape[0]
     part = k8 + 8
@@ -266,9 +297,16 @@
     out = pl.pallas_call(
         functools.partial(kernel, (n_row, n_col, c, h, w, k8)),
         out_shape=jax.ShapeDtypeStruct((c * h, w), F32),
-        in_specs=[vmem] * 9,
+        in_specs=[pl.BlockSpec(memory_space=pltpu.HBM)] * 9,
         out_specs=vmem,
         scratch_shapes=[
+            pltpu.VMEM((c * h, w), F32),
+            pltpu.VMEM((h, w), jnp.int32), pltpu.VMEM((h, w), jnp.int32), pltpu.VMEM((h, w), jnp.int32),
+            pltpu.VMEM(spread_rate.shape, F32),
+            pltpu.VMEM((c, c), F32), pltpu.VMEM((c, c), F32), pltpu.VMEM((c, c), F32),
+            pltpu.VMEM((1, c), F32),
+            pltpu.VMEM((2, c, w), F32),
+            pltpu.SemaphoreType.DMA((11,)),
             field, field, field, field, field, field,
             pltpu.VMEM((p_all + 2, w, two), F32),
             pltpu.VMEM((p_all, w + 2 * PAD, two), F32),
@@ -283,9 +321,9 @@
             pltpu.SemaphoreType.DMA((2, 4)),
             pltpu.SemaphoreType.DMA((2, 4)),
         ],
-        compiler_params=pltpu.CompilerParams(collective_id=0, has_side_effects=True, vmem_limit_bytes=48 * 1024 * 1024),
+        compiler_params=pltpu.CompilerParams(collective_id=0, has_side_effects=True, vmem_limit_bytes=56 * 1048576),
     )(
-        fire_state.reshape(c * h, w), fuel_class, firebreak, ignition,
+        fire_state, fuel_class, firebreak, ignition,
         spread_rate, spread_rows, spread_cols, reaction, ignition_heat.reshape(1, c),
     )
     return out.reshape(c, h, w)

time: 45.6 us -> 41.2 us (0.904); the launches traced: 45 us -> 41.1 us
  local copies, waits for them, and re-layouts: 8.39 us -> 2.65 us
  Pallas kernels: 36.6 us -> 38.4 us
    unnamed x19 -> x1, local copies, waits for them, and re-layouts: 8.39 us -> 2.65 us
    pallas_call x1, Pallas kernels: 36.6 us -> 38.4 us  [per_device(): pl.pallas_call(functools.partial(kernel, (n_row, n_col, c, h, w, k8)), ou...]
where the time goes in v1:
time: 41.2 us; the launch traced here: 41.1 us
  Pallas kernels  38.4 us (93%)
  local copies, waits for them, and re-layouts  2.65 us (6%)
    pallas_call x1, Pallas kernels, per_device(): pl.pallas_call(functools.partial(kernel, (n_row, n_col, c, h, w, k8)), ou...  38.4 us
    unnamed x1, local copies, waits for them, and re-layouts  2.65 us

profile of v1, /device:TPU:0, one launch (start us, length us, event | category | flops | bytes accessed | tf_op | source)
XLA Modules:
  0.0 41.1 jit_solution(6113752520916810222)
XLA Ops:
  0.0 38.4 %shard_map.91 = f32[3072,128]{1,0:T(8,128)} custom-call(f32[64,48,128]{2,1,0:T(8,128)} %x_hbm.1, s32[48,128]{1,0:T(8,128)} %fuel_hbm.1, s32[48,128]{1,0:T(8,128)} %break_hbm.1, s32[48,128]{1,0:T(8,128)} %lit_hbm.1, f32[13,64]{1,0:T(8,128)} %rate_hbm.1, f32[64,64]{1,0:T(8,128)} %srow_hbm.1, f32[64,64]{1,0:T(8,128)} %scol_hbm.1, f32[64,64]{1,0:T(8,128)} %react_hbm.1, ...), custom_call_target="tpu_custom_call" | custom-call | tf_op jit(solution)/shard_map/pallas_call | solution.py:297
  38.4 2.7 %copy.11 = f32[64,48,128]{2,1,0:T(8,128)} copy(f32[64,48,128]{2,1,0:T(8,128)} %bitcast.2) | data formatting | bytes 3145728

commit v2 on v1

--- a/solution.py
+++ b/solution.py
@@ -9,7 +9,7 @@
 
 ITERS = 4
 PAD = 8
-BLOCK = 4
+BLOCK = 12
 BF16, F32 = jnp.bfloat16, jnp.float32
 MESH = pl.DeviceIdType.MESH
 
@@ -93,11 +93,13 @@
         def _():
             copy(slot, d).start()
 
-    def finish(slot):
+    def sent(slot):
         for d in range(4):
             @pl.when(sends[d])
             def _(d=d):
                 copy(slot, d).wait_send()
+
+    def arrived(slot):
         for d in range(4):
             @pl.when(takes[d])
             def _(d=d):
@@ -267,13 +269,15 @@
 
     def step(i, carry):
         pointwise(v, False)
-        finish(0)
+        arrived(0)
         halo(0)
         combine(1, mid, False, None)
         pointwise(mid, True)
-        finish(1)
+        arrived(1)
         halo(1)
+        sent(0)
         combine(0, v, True, i == ITERS - 1)
+        sent(1)
         return carry
 
     lax.fori_loop(0, ITERS, step, 0)

time: 41.2 us -> 40.6 us (0.985)
  Pallas kernels: 38.4 us -> 37.8 us
    pallas_call x1, Pallas kernels: 38.4 us -> 37.8 us  [per_device(): pl.pallas_call(functools.partial(kernel, (n_row, n_col, c, h, w, k8)), ou...]
where the time goes in v2:
time: 40.6 us; the launch traced here: 40.4 us
  Pallas kernels  37.8 us (93%)
  local copies, waits for them, and re-layouts  2.65 us (7%)
    pallas_call x1, Pallas kernels, per_device(): pl.pallas_call(functools.partial(kernel, (n_row, n_col, c, h, w, k8)), ou...  37.8 us
    unnamed x1, local copies, waits for them, and re-layouts  2.65 us

profile of v2, /device:TPU:0, one launch (start us, length us, event | category | flops | bytes accessed | tf_op | source)
XLA Modules:
  0.0 40.4 jit_solution(13998948854522684369)
XLA Ops:
  0.0 37.8 %shard_map.91 = f32[3072,128]{1,0:T(8,128)} custom-call(f32[64,48,128]{2,1,0:T(8,128)} %x_hbm.1, s32[48,128]{1,0:T(8,128)} %fuel_hbm.1, s32[48,128]{1,0:T(8,128)} %break_hbm.1, s32[48,128]{1,0:T(8,128)} %lit_hbm.1, f32[13,64]{1,0:T(8,128)} %rate_hbm.1, f32[64,64]{1,0:T(8,128)} %srow_hbm.1, f32[64,64]{1,0:T(8,128)} %scol_hbm.1, f32[64,64]{1,0:T(8,128)} %react_hbm.1, ...), custom_call_target="tpu_custom_call" | custom-call | tf_op jit(solution)/shard_map/pallas_call | solution.py:301
  37.8 2.7 %copy.11 = f32[64,48,128]{2,1,0:T(8,128)} copy(f32[64,48,128]{2,1,0:T(8,128)} %bitcast.2) | data formatting | bytes 3145728
